TPU v7x, 32 devices: a whole 2x2x4 slice. The times are simulated.
32 devices in a mesh: ep: 8 (over z, y), dp: 4 (over x, core).
Axes of the slice: x: 2, y: 2, z: 4, core: 2. Of those that a mesh axis runs over, the one named last changes fastest.
Arguments:
- tokens: bfloat16 [4096, 2048], P(('dp', 'ep')), parts along dimension 0, may hold values from -6 to 6
- expert_ids: int32 [4096, 2], P(('dp', 'ep')), parts along dimension 0, may hold values from 0 to 7, all different within a row; in each aligned block of 128 rows (0 to 127, 128 to 255, ...) at most 48 rows name the same one
- gate_values: float32 [4096, 2], P(('dp', 'ep')), parts along dimension 0, may hold values from 0.1 to 1
- latent_down: bfloat16 [2048, 512], P('ep'), may hold values from -0.125 to 0.125
- latent_up: bfloat16 [512, 2048], P(None, 'ep'), may hold values from -0.25 to 0.25
- expert_up: bfloat16 [8, 512, 1408], P('ep'), may hold values from -0.25 to 0.25
- expert_down: bfloat16 [8, 1408, 512], P('ep'), may hold values from -0.15625 to 0.15625
- grad_out: bfloat16 [4096, 2048], P(('dp', 'ep')), parts along dimension 0, may hold values from -6 to 6
Outputs:
- layer_out: bfloat16 [4096, 2048], P(('dp', 'ep')), parts along dimension 0
- grad_tokens: bfloat16 [4096, 2048], P(('dp', 'ep')), parts along dimension 0
There are 4 independent parts, one for each index of `dp`. A program takes and returns all parts, laid end to end along the dimension named above; an argument that names none is the same for every part. Nothing has to cross between parts.
Inputs may be any that keep to these rules, and one draw needn't show every extreme that they name: `expert_ids`: each row names 2 different experts. Among the 128 tokens of one device, no expert is named by more than 48 tokens, and in every draw some expert is named by exactly 48 tokens of some device.
All inputs are finite; a program needn't handle non-finite values.
Results may differ from a plain program's by a relative error of at most 0.013.
Values may be sent and summed in bfloat16 or wider, within the bound.
A program may use at most 64 MiB of HBM per device.

v0:
```python
import jax
import jax.numpy as jnp
from jax import lax
from jax.sharding import PartitionSpec as P


def contract_last(left, right):
    return lax.dot_general(
        left, right, (((1,), (1,)), ((), ())), preferred_element_type=jnp.float32
    )


def on_device(
    tokens, expert_ids, gate_values, latent_down, latent_up, expert_up, expert_down, grad_out
):
    ep_size = lax.axis_size("ep")
    tok_rows = expert_ids.shape[0]
    top_count = expert_ids.shape[1]
    local_experts = expert_up.shape[0]
    width = latent_up.shape[0]
    experts = local_experts * ep_size
    capacity = max(2, (3 * tok_rows * top_count + 2 * experts - 1) // (2 * experts))
    full_down, full_up = (
        lax.all_gather(latent_down, "ep", axis=0, tiled=True),
        lax.all_gather(latent_up, "ep", axis=1, tiled=True),
    )
    latent = jnp.dot(tokens, full_down, preferred_element_type=jnp.float32).astype(jnp.bfloat16)
    numbers = jnp.arange(experts, dtype=jnp.int32)
    picked = (expert_ids[:, :, None] == numbers[None, None, :]).astype(jnp.int32)
    routed = jnp.sum(picked, axis=1)
    before = jnp.cumsum(routed, axis=0) - routed
    slot_pos = jnp.sum(picked * before[:, None, :], axis=2)
    flat_slot = expert_ids * capacity + slot_pos
    positions = jnp.arange(experts * capacity, dtype=jnp.int32)
    matches = flat_slot[None, :, :] == positions[:, None, None]
    placing = jnp.any(matches, axis=2).astype(jnp.bfloat16)
    gate_place = jnp.sum(jnp.where(matches, gate_values[None, :, :], 0.0), axis=2)
    outbound = jnp.dot(placing, latent, preferred_element_type=jnp.float32).astype(jnp.bfloat16)
    outbound = outbound.reshape(ep_size, local_experts, capacity, width)
    pre_act = jnp.einsum(
        "sjml,jlf->sjmf",
        lax.all_to_all(outbound, "ep", split_axis=0, concat_axis=0, tiled=True),
        expert_up,
        preferred_element_type=jnp.float32,
    )
    squared = jnp.square(jax.nn.relu(pre_act)).astype(jnp.bfloat16)
    expert_out = jnp.einsum(
        "sjmf,jfl->sjml", squared, expert_down, preferred_element_type=jnp.float32
    ).astype(jnp.bfloat16)
    expert_out, stored = (expert_out, pre_act)
    returned = lax.all_to_all(expert_out, "ep", split_axis=0, concat_axis=0, tiled=True).reshape(
        experts * capacity, width
    )
    gathered_rows = jnp.take(returned, flat_slot, axis=0)
    combined = jnp.sum(gate_values[:, :, None] * gathered_rows.astype(jnp.float32), axis=1).astype(
        jnp.bfloat16
    )
    layer_full = jnp.dot(combined, full_up, preferred_element_type=jnp.float32)
    grad_latent = contract_last(grad_out, full_up)
    layer_out = layer_full.astype(jnp.bfloat16)
    grad_send = jnp.dot(
        gate_place, grad_latent, precision=lax.Precision.HIGHEST, preferred_element_type=jnp.float32
    )
    grad_send = grad_send.astype(jnp.bfloat16).reshape(ep_size, local_experts, capacity, width)
    grad_arrived = lax.all_to_all(grad_send, "ep", split_axis=0, concat_axis=0, tiled=True)
    pre_act = stored
    grad_act = jnp.einsum(
        "sjml,jfl->sjmf", grad_arrived, expert_down, preferred_element_type=jnp.float32
    )
    grad_pre = (2.0 * jax.nn.relu(pre_act) * grad_act).astype(jnp.bfloat16)
    grad_in = jnp.einsum(
        "sjmf,jlf->sjml", grad_pre, expert_up, preferred_element_type=jnp.float32
    ).astype(jnp.bfloat16)
    grad_back = lax.all_to_all(grad_in, "ep", split_axis=0, concat_axis=0, tiled=True).reshape(
        experts * capacity, width
    )
    grad_sum = jnp.sum(jnp.take(grad_back, flat_slot, axis=0).astype(jnp.float32), axis=1).astype(
        jnp.bfloat16
    )
    grad_tokens = contract_last(grad_sum, full_down).astype(jnp.bfloat16)
    return (layer_out, grad_tokens)


def solution(mesh):
    placed = (
        P(("dp", "ep"), None),
        P(("dp", "ep"), None),
        P(("dp", "ep"), None),
        P("ep", None),
        P(None, "ep"),
        P("ep", None, None),
        P("ep", None, None),
        P(("dp", "ep"), None),
    )
    return jax.shard_map(
        on_device,
        mesh=mesh,
        in_specs=placed,
        out_specs=(P(("dp", "ep"), None), P(("dp", "ep"), None)),
        check_vma=False,
    )
```

profile of v0, /device:TPU:0, one launch (start us, length us, event | category | flops | bytes accessed | tf_op | source)
XLA Modules:
  0.0 187.3 jit_solution(12090486071343012626)
XLA Ops:
  9.7 0.8 select_reduce_fusion.1
  11.2 50.8 %all-gather.3.cloned.1.call-done = bf16[2048,512]{1,0:T(8,128)(2,1)} async-done(((bf16[256,512]{1,0:T(8,128)(2,1)}), bf16[2048,512]{1,0:T(8,128)(2,1)}) %all-gather.3.cloned.1.call-update) | async-done | bytes 2097168 | tf_op jit(solution)/shard_map/all_gather | solution.py:24
  62.0 3.2 %convolution_convert_fusion.3 = bf16[384,512]{1,0:T(8,128)(2,1)} fusion(pred[384,128]{1,0:T(8,128)(4,1)S(1)} %fusion.24, bf16[128,2048]{1,0:T(8,128)(2,1)} %param.10, bf16[2048,512]{1,0:T(8,128)(2,1)} %all-gather.3.cloned.1.call-done), kind=kOutput, calls=%fused_computation.17 | convolution fusion | flops 319029248 | bytes 3063808 | tf_op jit(solution)/shard_map/dot_general | solution.py:38
  65.2 3.5 %all-to-all-start = ((bf16[8,1,48,512]{3,2,1,0:T(8,128)(2,1)}), bf16[8,1,48,512]{3,2,1,0:T(8,128)(2,1)S(1)}, u32[]{:S(2)}, u32[]{:S(2)}) async-start(bf16[8,1,48,512]{3,2,1,0:T(8,128)(2,1)} %bitcast.1), calls=%async_computation | async-start | bytes 786432 | tf_op jit(solution)/shard_map/all_to_all | solution.py:42
  68.7 47.1 %all-gather.5.cloned.1.call-done = bf16[512,2048]{1,0:T(8,128)(2,1)} async-done(((bf16[512,256]{1,0:T(8,128)(2,1)}), bf16[512,2048]{1,0:T(8,128)(2,1)}) %all-gather.5.cloned.1.call-update) | async-done | bytes 2097168 | tf_op jit(solution)/shard_map/all_gather | solution.py:25
  115.8 2.4 %fusion.28 = f32[128,512]{1,0:T(8,128)S(1)} fusion(bf16[128,2048]{1,0:T(8,128)(2,1)S(1)} %copy-done.3, bf16[512,2048]{1,0:T(8,128)(2,1)} %all-gather.5.cloned.1.call-done), kind=kOutput, calls=%fused_computation.39 | convolution fusion | flops 268435456 | bytes 2883584 | tf_op jit(solution)/shard_map/dot_general | solution.py:8
  118.2 1.5 convolution_convert_fusion.2
  119.8 4.1 %all-to-all-start.2 = ((bf16[8,1,48,512]{3,2,1,0:T(8,128)(2,1)}), bf16[8,1,48,512]{3,2,1,0:T(8,128)(2,1)}, u32[]{:S(2)}, u32[]{:S(2)}) async-start(bf16[8,1,48,512]{3,2,1,0:T(8,128)(2,1)} %bitcast.13), calls=%async_computation.2 | async-start | bytes 786432 | tf_op jit(solution)/shard_map/all_to_all | solution.py:65
  123.9 2.1 %convolution_maximum_fusion = f32[8,48,1408]{2,1,0:T(8,128)} fusion(bf16[1,512,1408]{2,1,0:T(8,128)(2,1)S(1)} %copy-done, bf16[8,1,48,512]{3,2,1,0:T(8,128)(2,1)S(1)} %all-to-all-done), kind=kOutput, calls=%fused_computation.3 | convolution fusion | flops 554188800 | bytes 3997696 | tf_op jit(solution)/shard_map/sjml,jlf->sjmf/dot_general | solution.py:40
  126.0 9.0 %all-to-all-done.2 = bf16[8,1,48,512]{3,2,1,0:T(8,128)(2,1)} async-done(((bf16[8,1,48,512]{3,2,1,0:T(8,128)(2,1)}), bf16[8,1,48,512]{3,2,1,0:T(8,128)(2,1)}, u32[]{:S(2)}, u32[]{:S(2)}) %all-to-all-start.2) | async-done | bytes 393248 | tf_op jit(solution)/shard_map/all_to_all | solution.py:65
  135.0 3.9 %fusion.16 = bf16[8,1,48,512]{3,2,1,0:T(8,128)(2,1)} fusion(bf16[1,512,1408]{2,1,0:T(8,128)(2,1)S(1)} %copy-done, f32[8,48,1408]{2,1,0:T(8,128)} %convolution_maximum_fusion, bf16[1,1408,512]{2,1,0:T(8,128)(2,1)S(1)} %copy-done.2, bf16[8,1,48,512]{3,2,1,0:T(8,128)(2,1)} %all-to-all-done.2), kind=kOutput, calls=%fused_computation.19 | convolution fusion | flops 1109114880 | bytes 5832704 | tf_op jit(solution)/shard_map/sjmf,jlf->sjml/dot_general | solution.py:71
  138.9 3.6 %all-to-all-start.3 = ((bf16[8,1,48,512]{3,2,1,0:T(8,128)(2,1)}), bf16[8,1,48,512]{3,2,1,0:T(8,128)(2,1)S(1)}, u32[]{:S(2)}, u32[]{:S(2)}) async-start(bf16[8,1,48,512]{3,2,1,0:T(8,128)(2,1)} %fusion.16), calls=%async_computation.3 | async-start | bytes 786432 | tf_op jit(solution)/shard_map/all_to_all | solution.py:74
  142.5 3.1 %fusion.13 = bf16[8,1,48,512]{3,2,1,0:T(8,128)(2,1)} fusion(bf16[1,1408,512]{2,1,0:T(8,128)(2,1)S(1)} %copy-done.2, f32[8,48,1408]{2,1,0:T(8,128)} %convolution_maximum_fusion), kind=kOutput, calls=%fused_computation.18 | convolution fusion | flops 554926080 | bytes 3997696 | tf_op jit(solution)/shard_map/sjmf,jfl->sjml/dot_general | solution.py:47
  145.7 7.9 %all-to-all-done.3 = bf16[8,1,48,512]{3,2,1,0:T(8,128)(2,1)S(1)} async-done(((bf16[8,1,48,512]{3,2,1,0:T(8,128)(2,1)}), bf16[8,1,48,512]{3,2,1,0:T(8,128)(2,1)S(1)}, u32[]{:S(2)}, u32[]{:S(2)}) %all-to-all-start.3) | async-done | bytes 393248 | tf_op jit(solution)/shard_map/all_to_all | solution.py:74
  153.6 3.7 %all-to-all-start.1 = ((bf16[8,1,48,512]{3,2,1,0:T(8,128)(2,1)}), bf16[8,1,48,512]{3,2,1,0:T(8,128)(2,1)S(1)}, u32[]{:S(2)}, u32[]{:S(2)}) async-start(bf16[8,1,48,512]{3,2,1,0:T(8,128)(2,1)} %fusion.13), calls=%async_computation.1 | async-start | bytes 786432 | tf_op jit(solution)/shard_map/all_to_all | solution.py:51
  158.4 1.2 gather_fusion.1
  159.6 0.8 reshape.102
  160.4 8.4 %all-to-all-done.1 = bf16[8,1,48,512]{3,2,1,0:T(8,128)(2,1)S(1)} async-done(((bf16[8,1,48,512]{3,2,1,0:T(8,128)(2,1)}), bf16[8,1,48,512]{3,2,1,0:T(8,128)(2,1)S(1)}, u32[]{:S(2)}, u32[]{:S(2)}) %all-to-all-start.1) | async-done | bytes 393248 | tf_op jit(solution)/shard_map/all_to_all | solution.py:51
  168.8 1.9 gather_fusion
  170.6 1.9 %reshape.98 = bf16[128,2,512]{2,1,0:T(2,128)(2,1)} reshape(bf16[256,512]{1,0:T(8,128)(2,1)} %gather_fusion) | data formatting | bytes 524288 | tf_op jit(solution)/shard_map/jit(_take)/gather | solution.py:54
  172.5 1.6 fusion.25
  174.1 1.8 multiply_reduce_fusion
  176.0 3.2 %convolution_convert_fusion = bf16[128,2048]{1,0:T(8,128)(2,1)} fusion(bf16[128,512]{1,0:T(8,128)(2,1)S(1)} %fusion.25, bf16[2048,512]{1,0:T(8,128)(2,1)} %all-gather.3.cloned.1.call-done), kind=kOutput, calls=%fused_computation.5 | convolution fusion | flops 268697600 | bytes 2752512 | tf_op jit(solution)/shard_map/dot_general | solution.py:8
  179.2 1.3 convolution_convert_fusion.1
  (29 shorter events, 4.4 us)
Async XLA Ops:
  7.2 116.7 %copy-start = (bf16[1,512,1408]{2,1,0:T(8,128)(2,1)S(1)}, bf16[1,512,1408]{2,1,0:T(8,128)(2,1)}, u32[]{:S(2)}) copy-start(bf16[1,512,1408]{2,1,0:T(8,128)(2,1)} %param.15) | copy-start | bytes 4325380
  7.2 54.8 %all-gather.3.cloned.1.call-start = ((), (), s32[]{:S(2)}) async-start(), calls=%async_computation.4 | async-start | bytes 2359296 | tf_op jit(solution)/shard_map/all_gather | solution.py:24
  7.9 107.9 %all-gather.5.cloned.1.call-start = ((), (), s32[]{:S(2)}) async-start(), calls=%async_computation.5 | async-start | bytes 2359296 | tf_op jit(solution)/shard_map/all_gather | solution.py:25
  9.6 59.0 %copy-start.4 = (f32[128,2]{0,1:T(2,128)S(1)}, f32[128,2]{0,1:T(2,128)}, u32[]{:S(2)}) copy-start(f32[128,2]{0,1:T(2,128)} %param.12) | copy-start | bytes 3076
  9.6 106.2 %copy-start.3 = (bf16[128,2048]{1,0:T(8,128)(2,1)S(1)}, bf16[128,2048]{1,0:T(8,128)(2,1)}, u32[]{:S(2)}) copy-start(bf16[128,2048]{1,0:T(8,128)(2,1)} %param.17) | copy-start | bytes 1572868
  65.2 54.6 %all-to-all-start = ((bf16[8,1,48,512]{3,2,1,0:T(8,128)(2,1)}), bf16[8,1,48,512]{3,2,1,0:T(8,128)(2,1)S(1)}, u32[]{:S(2)}, u32[]{:S(2)}) async-start(bf16[8,1,48,512]{3,2,1,0:T(8,128)(2,1)} %bitcast.1), calls=%async_computation | async-start | bytes 786432 | tf_op jit(solution)/shard_map/all_to_all | solution.py:42
  119.8 15.2 %all-to-all-start.2 = ((bf16[8,1,48,512]{3,2,1,0:T(8,128)(2,1)}), bf16[8,1,48,512]{3,2,1,0:T(8,128)(2,1)}, u32[]{:S(2)}, u32[]{:S(2)}) async-start(bf16[8,1,48,512]{3,2,1,0:T(8,128)(2,1)} %bitcast.13), calls=%async_computation.2 | async-start | bytes 786432 | tf_op jit(solution)/shard_map/all_to_all | solution.py:65
  123.9 11.1 %copy-start.2 = (bf16[1,1408,512]{2,1,0:T(8,128)(2,1)S(1)}, bf16[1,1408,512]{2,1,0:T(8,128)(2,1)}, u32[]{:S(2)}) copy-start(bf16[1,1408,512]{2,1,0:T(8,128)(2,1)} %param.16) | copy-start | bytes 4325380
  138.9 14.7 %all-to-all-start.3 = ((bf16[8,1,48,512]{3,2,1,0:T(8,128)(2,1)}), bf16[8,1,48,512]{3,2,1,0:T(8,128)(2,1)S(1)}, u32[]{:S(2)}, u32[]{:S(2)}) async-start(bf16[8,1,48,512]{3,2,1,0:T(8,128)(2,1)} %fusion.16), calls=%async_computation.3 | async-start | bytes 786432 | tf_op jit(solution)/shard_map/all_to_all | solution.py:74
  153.6 15.2 %all-to-all-start.1 = ((bf16[8,1,48,512]{3,2,1,0:T(8,128)(2,1)}), bf16[8,1,48,512]{3,2,1,0:T(8,128)(2,1)S(1)}, u32[]{:S(2)}, u32[]{:S(2)}) async-start(bf16[8,1,48,512]{3,2,1,0:T(8,128)(2,1)} %fusion.13), calls=%async_computation.1 | async-start | bytes 786432 | tf_op jit(solution)/shard_map/all_to_all | solution.py:51
  170.6 8.6 %copy-start.1 = (bf16[512,2048]{1,0:T(8,128)(2,1)S(1)}, bf16[512,2048]{1,0:T(8,128)(2,1)}, u32[]{:S(2)}) copy-start(bf16[512,2048]{1,0:T(8,128)(2,1)} %all-gather.5.cloned.1.call-done) | copy-start | bytes 6291460
Sparse Core Ops, SparseCore 0:
  10.1 51.7 all-gather.2
  64.0 51.7 all-gather.4
where the time goes:
time: 188 us; the launch traced here: 187 us
  waiting for transfers between devices  125 us (66%)
  matrix products  20.8 us (11%)
  starting transfers between devices  14.9 us (8%)
  between operations  14.2 us (8%)
  local copies, waits for them, and re-layouts  7 us (4%)
  other arithmetic  5.84 us (3%)
    all_gather x1, waiting for transfers between devices, on_device(): lax.all_gather(latent_down, 'ep', axis=0, tiled=True)  50.8 us
    all_gather x1, waiting for transfers between devices, on_device(): lax.all_gather(latent_up, 'ep', axis=1, tiled=True)  47.1 us
    all_to_all x1, waiting for transfers between devices, on_device(): lax.all_to_all(grad_send, 'ep', split_axis=0, concat_axis=0, tiled=True)  8.96 us
    all_to_all x1, waiting for transfers between devices, on_device(): lax.all_to_all(expert_out, 'ep', split_axis=0, concat_axis=0, tiled=True)  8.42 us
    all_to_all x1, waiting for transfers between devices, on_device(): lax.all_to_all(grad_in, 'ep', split_axis=0, concat_axis=0, tiled=True)  7.91 us
    dot_general x2, matrix products, contract_last(): lax.dot_general(left, right, (((1,), (1,)), ((), ())), preferred_element_...  5.62 us
    all_to_all x1, starting transfers between devices, on_device(): lax.all_to_all(grad_send, 'ep', split_axis=0, concat_axis=0, tiled=True)  4.1 us
    dot_general x1, matrix products, on_device(): jnp.einsum('sjmf,jlf->sjml', grad_pre, expert_up, preferred_element_type=...  3.91 us
  transfers between devices with their start and end apart: 6, of which 5 were waited for; matrix products, arithmetic and copies ran while one was open for 10% of the time, Pallas kernels for 0%

commit v1 on v0

v1 whole, which is shorter than its diff:
```python
import functools

import jax
import jax.numpy as jnp
from jax import lax
from jax.experimental import pallas as pl
from jax.experimental.pallas import tpu as pltpu
from jax.sharding import PartitionSpec as P

MESH = pl.DeviceIdType.MESH
ROW_TILE = 16

DOWN, UP, LATENT, GRAD, FORWARD, BACKWARD, DOWN_TWIN, UP_TWIN = range(8)


def dot(left, right):
    return jnp.dot(left, right, preferred_element_type=jnp.float32)


def contract_last(left, right):
    return lax.dot_general(
        left, right, (((1,), (1,)), ((), ())), preferred_element_type=jnp.float32
    )


def kernel(
    ep_size,
    share,
    slots,
    ids_ref,
    gates_ref,
    tokens_hbm,
    grad_out_hbm,
    down_hbm,
    up_hbm,
    expert_up_hbm,
    expert_down_hbm,
    layer_ref,
    grad_ref,
    tokens,
    grad_out,
    expert_up,
    expert_down,
    full_down,
    full_up,
    lat_send,
    lat_recv,
    grad_send,
    grad_recv,
    pre_act,
    out_send,
    out_recv,
    in_send,
    in_recv,
    local_sem,
    send_sem,
    recv_sem,
):
    me = lax.axis_index("ep")
    row = lax.axis_index("dp")
    twin = row + 1 - 2 * lax.rem(row, 2)
    part = lax.rem(row, 2) if share == 2 else 0
    other = 1 - part
    shard = down_hbm.shape[0]
    piece = shard // share
    tok_rows = tokens.shape[0]
    total = lat_send.shape[0]
    bf16 = jnp.bfloat16

    def peers(body):
        lax.fori_loop(1, ep_size, lambda d, c: (body(d), c)[1], 0)

    def after(d):
        return lax.rem(me + d, ep_size)

    def ahead(d):
        return lax.rem(me + ep_size - d, ep_size)

    loads = [
        pltpu.make_async_copy(src, dst, local_sem.at[i])
        for i, (src, dst) in enumerate(
            (
                (tokens_hbm, tokens),
                (grad_out_hbm, grad_out),
                (expert_up_hbm.at[0], expert_up),
                (expert_down_hbm.at[0], expert_down),
                (down_hbm, full_down.at[pl.ds(pl.multiple_of(me * shard, ROW_TILE), shard)]),
                (up_hbm, full_up.at[pl.ds(pl.multiple_of(me * shard, ROW_TILE), shard)]),
            )
        )
    ]
    for load in loads:
        load.start()

    barrier = pltpu.get_barrier_semaphore()

    def greet(d):
        pl.semaphore_signal(barrier, inc=1, device_id={"ep": after(d)}, device_id_type=MESH)

    peers(greet)
    if share == 2:
        pl.semaphore_signal(barrier, inc=1, device_id={"dp": twin}, device_id_type=MESH)
    pl.semaphore_wait(barrier, ep_size - 1 + (share - 1))

    def piece_at(owner, which):
        return pl.ds(pl.multiple_of(owner * shard + which * piece, ROW_TILE), piece)

    def gather_copy(kind, src, full, owner, peer):
        return pltpu.make_async_remote_copy(
            src_ref=src.at[pl.ds(pl.multiple_of(part * piece, ROW_TILE), piece)],
            dst_ref=full.at[piece_at(owner, part)],
            send_sem=send_sem.at[kind, peer],
            recv_sem=recv_sem.at[kind, owner],
            device_id={"ep": peer},
            device_id_type=MESH,
        )

    def twin_copy(kind, full, owner, which):
        return pltpu.make_async_remote_copy(
            src_ref=full.at[piece_at(owner, which)],
            dst_ref=full.at[piece_at(owner, which)],
            send_sem=send_sem.at[kind, owner],
            recv_sem=recv_sem.at[kind, owner],
            device_id={"dp": twin},
            device_id_type=MESH,
        )

    peers(lambda d: gather_copy(DOWN, down_hbm, full_down, me, after(d)).start())
    peers(lambda d: gather_copy(UP, up_hbm, full_up, me, after(d)).start())

    def slot_at(index):
        return pl.ds(pl.multiple_of(index * slots, ROW_TILE), slots)

    def exchange_copy(kind, send, recv, peer, owner):
        return pltpu.make_async_remote_copy(
            src_ref=send.at[slot_at(peer)],
            dst_ref=recv.at[slot_at(owner)],
            send_sem=send_sem.at[kind, peer],
            recv_sem=recv_sem.at[kind, owner],
            device_id={"ep": peer},
            device_id_type=MESH,
        )

    def own_copy(kind, send, recv):
        return pltpu.make_async_copy(
            send.at[slot_at(me)], recv.at[slot_at(me)], recv_sem.at[kind, me]
        )

    def exchange_start(kind, send, recv):
        peers(lambda d: exchange_copy(kind, send, recv, after(d), me).start())
        own_copy(kind, send, recv).start()

    def exchange_wait(kind, send, recv):
        own_copy(kind, send, recv).wait()
        peers(lambda d: exchange_copy(kind, send, recv, after(d), ahead(d)).wait_recv())

    ids = ids_ref[...]
    gates = gates_ref[...]
    choices = ids.shape[1]
    lanes = lax.broadcasted_iota(jnp.int32, (tok_rows, ep_size), 1)
    picks = [(ids[:, k : k + 1] == lanes).astype(jnp.float32) for k in range(choices)]
    routed = functools.reduce(jnp.add, picks)
    lower = (
        lax.broadcasted_iota(jnp.int32, (tok_rows, tok_rows), 1)
        < lax.broadcasted_iota(jnp.int32, (tok_rows, tok_rows), 0)
    ).astype(bf16)
    before = dot(lower, routed.astype(bf16))
    by_token = lax.broadcasted_iota(jnp.int32, (tok_rows, total), 1)
    by_slot = lax.broadcasted_iota(jnp.int32, (total, tok_rows), 0)
    take, place = [], []
    for k in range(choices):
        pos = jnp.sum(picks[k] * before, axis=1, keepdims=True)
        flat = ids[:, k : k + 1].astype(jnp.float32) * slots + pos
        take.append((flat.astype(jnp.int32) == by_token).astype(bf16))
        flat_row = jnp.transpose(jnp.broadcast_to(flat, (tok_rows, tok_rows)))[0:1, :]
        place.append((flat_row.astype(jnp.int32) == by_slot).astype(bf16))

    def gather_wait(kind, twin_kind, src, full, first, last):
        def arrive(d, c):
            gather_copy(kind, src, full, ahead(d), after(d)).wait_recv()
            if share == 2:
                twin_copy(twin_kind, full, ahead(d), part).start()
            return c

        lax.fori_loop(first, last, arrive, 0)

    def twin_wait(twin_kind, full):
        if share == 2:
            peers(lambda d: twin_copy(twin_kind, full, ahead(d), other).wait_recv())

    gather_wait(DOWN, DOWN_TWIN, down_hbm, full_down, 1, ep_size)
    loads[0].wait()
    loads[4].wait()
    twin_wait(DOWN_TWIN, full_down)
    latent = dot(tokens[...], full_down[...]).astype(bf16)
    lat_send[...] = dot(functools.reduce(jnp.add, place), latent).astype(bf16)
    exchange_start(LATENT, lat_send, lat_recv)

    middle = 1 + ep_size // 2
    gather_wait(UP, UP_TWIN, up_hbm, full_up, 1, middle)

    rows = total if total <= 512 else 256
    blocks = total // rows

    def each_block(body):
        if blocks == 1:
            body(slice(None))
        else:
            lax.fori_loop(
                0,
                blocks,
                lambda b, c: (body(pl.ds(pl.multiple_of(b * rows, ROW_TILE), rows)), c)[1],
                0,
            )

    def forward(at):
        hidden = jnp.maximum(dot(lat_recv[at, :], expert_up[...]), 0.0)
        pre_act[at, :] = hidden
        out_send[at, :] = dot((hidden * hidden).astype(bf16), expert_down[...]).astype(bf16)

    loads[2].wait()
    loads[3].wait()
    exchange_wait(LATENT, lat_send, lat_recv)
    each_block(forward)
    exchange_start(FORWARD, out_send, out_recv)

    gather_wait(UP, UP_TWIN, up_hbm, full_up, middle, ep_size)
    loads[1].wait()
    loads[5].wait()
    twin_wait(UP_TWIN, full_up)
    grad_latent = dot(grad_out[...], full_up[...])
    sent = [
        dot(place[k], (gates[:, k : k + 1] * grad_latent).astype(bf16)) for k in range(choices)
    ]
    grad_send[...] = functools.reduce(jnp.add, sent).astype(bf16)
    exchange_start(GRAD, grad_send, grad_recv)

    exchange_wait(FORWARD, out_send, out_recv)
    returned = out_recv[...]
    combined = functools.reduce(
        jnp.add, [gates[:, k : k + 1] * dot(take[k], returned) for k in range(choices)]
    ).astype(bf16)
    layer_ref[...] = contract_last(combined, full_up[...]).astype(bf16)

    def backward(at):
        grad_act = contract_last(grad_recv[at, :], expert_down[...])
        grad_pre = (2.0 * pre_act[at, :] * grad_act).astype(bf16)
        in_send[at, :] = contract_last(grad_pre, expert_up[...]).astype(bf16)

    exchange_wait(GRAD, grad_send, grad_recv)
    each_block(backward)
    exchange_start(BACKWARD, in_send, in_recv)
    exchange_wait(BACKWARD, in_send, in_recv)
    grad_sum = dot(functools.reduce(jnp.add, take), in_recv[...]).astype(bf16)
    grad_ref[...] = contract_last(grad_sum, full_down[...]).astype(bf16)

    def finish(d):
        gather_copy(DOWN, down_hbm, full_down, me, after(d)).wait_send()
        gather_copy(UP, up_hbm, full_up, me, after(d)).wait_send()
        exchange_copy(LATENT, lat_send, lat_recv, after(d), me).wait_send()
        exchange_copy(GRAD, grad_send, grad_recv, after(d), me).wait_send()
        exchange_copy(FORWARD, out_send, out_recv, after(d), me).wait_send()
        exchange_copy(BACKWARD, in_send, in_recv, after(d), me).wait_send()
        if share == 2:
            twin_copy(DOWN_TWIN, full_down, after(d), part).wait_send()
            twin_copy(UP_TWIN, full_up, after(d), part).wait_send()

    peers(finish)


def on_device(
    tokens, expert_ids, gate_values, latent_down, latent_up, expert_up, expert_down, grad_out
):
    ep_size = lax.axis_size("ep")
    dp_size = lax.axis_size("dp")
    tok_rows, model = tokens.shape
    top_count = expert_ids.shape[1]
    local_experts, width, hidden = expert_up.shape
    assert local_experts == 1
    experts = local_experts * ep_size
    capacity = max(2, (3 * tok_rows * top_count + 2 * experts - 1) // (2 * experts))
    slots = (capacity + ROW_TILE - 1) // ROW_TILE * ROW_TILE
    total = experts * slots
    shard = latent_down.shape[0]
    share = 2 if dp_size % 2 == 0 and shard % (2 * ROW_TILE) == 0 else 1
    bf16 = jnp.bfloat16
    buffer = pltpu.VMEM((total, width), bf16)
    vmem = pl.BlockSpec(memory_space=pltpu.VMEM)
    anywhere = pl.BlockSpec(memory_space=pl.ANY)
    return pl.pallas_call(
        functools.partial(kernel, ep_size, share, slots),
        out_shape=[jax.ShapeDtypeStruct((tok_rows, model), bf16)] * 2,
        in_specs=[vmem, vmem] + [anywhere] * 6,
        out_specs=[vmem, vmem],
        scratch_shapes=[
            pltpu.VMEM((tok_rows, model), bf16),
            pltpu.VMEM((tok_rows, model), bf16),
            pltpu.VMEM((width, hidden), bf16),
            pltpu.VMEM((hidden, width), bf16),
            pltpu.VMEM((model, width), bf16),
            pltpu.VMEM((model, width), bf16),
            buffer,
            buffer,
            buffer,
            buffer,
            pltpu.VMEM((total, hidden), jnp.float32),
            buffer,
            buffer,
            buffer,
            buffer,
            pltpu.SemaphoreType.DMA((6,)),
            pltpu.SemaphoreType.DMA((8, ep_size)),
            pltpu.SemaphoreType.DMA((8, ep_size)),
        ],
        compiler_params=pltpu.CompilerParams(
            collective_id=0, has_side_effects=True, vmem_limit_bytes=60 * 1024 * 1024
        ),
    )(
        expert_ids,
        gate_values,
        tokens,
        grad_out,
        latent_down,
        latent_up.T,
        expert_up,
        expert_down,
    )


def solution(mesh):
    placed = (
        P(("dp", "ep"), None),
        P(("dp", "ep"), None),
        P(("dp", "ep"), None),
        P("ep", None),
        P(None, "ep"),
        P("ep", None, None),
        P("ep", None, None),
        P(("dp", "ep"), None),
    )
    return jax.shard_map(
        on_device,
        mesh=mesh,
        in_specs=placed,
        out_specs=(P(("dp", "ep"), None), P(("dp", "ep"), None)),
        check_vma=False,
    )
```

time: 188 us -> 104 us (0.55)
  waiting for transfers between devices: 125 us -> 0 us
  Pallas kernels: 0 us -> 94.4 us
  matrix products: 20.8 us -> 0 us
  starting transfers between devices: 14.9 us -> 0 us
  between operations: 14.2 us -> 0.64 us
  other arithmetic: 5.84 us -> 0 us
    all_gather x2 -> x0, waiting for transfers between devices: 97.9 us -> none  [the longest x1 50.8 us: on_device(): lax.all_gather(latent_down, 'ep', axis=0, tiled=True)]
    pallas_call x0 -> x1, Pallas kernels: none -> 94.4 us  [on_device(): pl.pallas_call(functools.partial(kernel, ep_size, share, slots), out_shap...]
    all_to_all x4 -> x0, waiting for transfers between devices: 25.3 us -> none  [the longest x1 8.96 us: on_device(): lax.all_to_all(grad_send, 'ep', split_axis=0, concat_axis=0, tiled=True)]
    dot_general x8 -> x0, matrix products: 20.8 us -> none  [the longest x2 5.62 us: contract_last(): lax.dot_general(left, right, (((1,), (1,)), ((), ())), preferred_element_...]
    all_to_all x4 -> x0, starting transfers between devices: 14.9 us -> none  [the longest x1 4.1 us: on_device(): lax.all_to_all(grad_send, 'ep', split_axis=0, concat_axis=0, tiled=True)]
    unnamed x11 -> x5, local copies, waits for them, and re-layouts: 0.76 us -> 8.38 us
    gather x4 -> x0, local copies, waits for them, and re-layouts: 5.7 us -> none  [the longest x2 3.76 us: on_device(): gathered_rows = jnp.take(returned, flat_slot, axis=0)]
    reduce_sum x5 -> x0, other arithmetic: 4.92 us -> none  [the longest x1 1.83 us: on_device(): jnp.sum(gate_values[:, :, None] * gathered_rows.astype(jnp.float32), axis=1)]
  transfers between devices with their start and end apart: 6 -> 0, of which waited for: 5 -> 0; matrix products, arithmetic and copies ran while one was open for 10% -> 0% of each run, Pallas kernels for 0% -> 0%
where the time goes in v1:
time: 104 us; the launch traced here: 103 us
  Pallas kernels  94.4 us (91%)
  local copies, waits for them, and re-layouts  8.38 us (8%)
    pallas_call x1, Pallas kernels, on_device(): pl.pallas_call(functools.partial(kernel, ep_size, share, slots), out_shap...  94.4 us
    unnamed x5, local copies, waits for them, and re-layouts  8.38 us

profile of v1, /device:TPU:0, one launch (start us, length us, event | category | flops | bytes accessed | tf_op | source)
XLA Modules:
  0.0 103.5 jit_solution(5361332279662244502)
XLA Ops:
  0.6 1.4 %copy.11.ids_ref = s32[128,2]{1,0:T(8,128)} copy(s32[128,2]{0,1:T(2,128)} %param.9) | data formatting | bytes 2048 | tf_op args[1]
  2.0 1.4 %copy.12.gates_ref = f32[128,2]{1,0:T(8,128)} copy(f32[128,2]{0,1:T(2,128)} %param.10) | data formatting | bytes 2048 | tf_op args[2]
  3.5 1.8 %copy.10 = bf16[512,256]{0,1:T(8,128)(2,1)} copy(bf16[512,256]{1,0:T(8,128)(2,1)} %param.12) | data formatting | bytes 524288 | tf_op args[4]
  5.3 94.4 %shard_map.95 = (bf16[128,2048]{1,0:T(8,128)(2,1)}, bf16[128,2048]{1,0:T(8,128)(2,1)}) custom-call(s32[128,2]{1,0:T(8,128)} %copy.11.ids_ref, f32[128,2]{1,0:T(8,128)} %copy.12.gates_ref, bf16[128,2048]{1,0:T(8,128)(2,1)} %tokens_hbm.1, bf16[128,2048]{1,0:T(8,128)(2,1)} %grad_out_hbm.1, bf16[256,512]{1,0:T(8,128)(2,1)} %down_hbm.1, ...), custom_call_target="tpu_custom_call" | custom-call | tf_op jit(solution)/shard_map/pallas_call | solution.py:290
  99.7 1.9 %copy.15 = bf16[128,2048]{1,0:T(8,128)(2,1)} copy(bf16[128,2048]{1,0:T(8,128)(2,1)} %get-tuple-element.4) | data formatting | bytes 1048576
  101.6 1.9 %copy.16 = bf16[128,2048]{1,0:T(8,128)(2,1)} copy(bf16[128,2048]{1,0:T(8,128)(2,1)} %get-tuple-element.5) | data formatting | bytes 1048576

commit v2 on v1

--- a/solution.py
+++ b/solution.py
@@ -10,7 +10,9 @@
 MESH = pl.DeviceIdType.MESH
 ROW_TILE = 16
 
-DOWN, UP, LATENT, GRAD, FORWARD, BACKWARD, DOWN_TWIN, UP_TWIN = range(8)
+UPWARD, DOWNWARD, ACROSS, TWIN = range(4)
+LATENT, GRAD, FORWARD, BACKWARD = range(4)
+SEND_BASE, RECV_BASE = 8, 4
 
 
 def dot(left, right):
@@ -43,6 +45,7 @@
     expert_down,
     full_down,
     full_up,
+    up_shard,
     lat_send,
     lat_recv,
     grad_send,
@@ -85,7 +88,7 @@
                 (expert_up_hbm.at[0], expert_up),
                 (expert_down_hbm.at[0], expert_down),
                 (down_hbm, full_down.at[pl.ds(pl.multiple_of(me * shard, ROW_TILE), shard)]),
-                (up_hbm, full_up.at[pl.ds(pl.multiple_of(me * shard, ROW_TILE), shard)]),
+                (up_hbm, up_shard),
             )
         )
     ]
@@ -105,28 +108,114 @@
     def piece_at(owner, which):
         return pl.ds(pl.multiple_of(owner * shard + which * piece, ROW_TILE), piece)
 
-    def gather_copy(kind, src, full, owner, peer):
+    full = (full_down, full_up)
+    height = ep_size // 2
+    level = me // 2
+    side = lax.rem(me, 2)
+
+    def piece_copy(m, owner, which, target, row_of, from_twin=0):
         return pltpu.make_async_remote_copy(
-            src_ref=src.at[pl.ds(pl.multiple_of(part * piece, ROW_TILE), piece)],
-            dst_ref=full.at[piece_at(owner, part)],
-            send_sem=send_sem.at[kind, peer],
-            recv_sem=recv_sem.at[kind, owner],
-            device_id={"ep": peer},
+            src_ref=full[m].at[piece_at(owner, which)],
+            dst_ref=full[m].at[piece_at(owner, which)],
+            send_sem=send_sem.at[4 * m + row_of, owner],
+            recv_sem=recv_sem.at[2 * m + from_twin, owner],
+            device_id=target,
             device_id_type=MESH,
         )
 
-    def twin_copy(kind, full, owner, which):
-        return pltpu.make_async_remote_copy(
-            src_ref=full.at[piece_at(owner, which)],
-            dst_ref=full.at[piece_at(owner, which)],
-            send_sem=send_sem.at[kind, owner],
-            recv_sem=recv_sem.at[kind, owner],
-            device_id={"dp": twin},
-            device_id_type=MESH,
-        )
-
-    peers(lambda d: gather_copy(DOWN, down_hbm, full_down, me, after(d)).start())
-    peers(lambda d: gather_copy(UP, up_hbm, full_up, me, after(d)).start())
+    def upward(m, owner):
+        return piece_copy(m, owner, part, {"ep": me + 2}, UPWARD)
+
+    def downward(m, owner):
+        return piece_copy(m, owner, part, {"ep": me - 2}, DOWNWARD)
+
+    def across(m, owner):
+        return piece_copy(m, owner, part, {"ep": me + 1 - 2 * side}, ACROSS)
+
+    def to_twin(m, owner, which):
+        return piece_copy(m, owner, which, {"dp": twin}, TWIN, 1)
+
+    def own_each(m, act):
+        @pl.when(level + 1 < height)
+        def _():
+            act(upward(m, me))
+
+        @pl.when(level > 0)
+        def _():
+            act(downward(m, me))
+
+        act(across(m, me))
+
+    def relay_each(m, d, act, arrive):
+        @pl.when(level >= d)
+        def _():
+            owner = me - 2 * d
+            arrive(m, owner)
+
+            @pl.when(level + 1 < height)
+            def _():
+                act(upward(m, owner))
+
+            act(across(m, owner))
+            if share == 2:
+                act(to_twin(m, owner, part))
+
+        @pl.when(level + d < height)
+        def _():
+            owner = me + 2 * d
+            arrive(m, owner)
+
+            @pl.when(level > 0)
+            def _():
+                act(downward(m, owner))
+
+            act(across(m, owner))
+            if share == 2:
+                act(to_twin(m, owner, part))
+
+    def cross_each(m, d, act, arrive):
+        partner = me + 1 - 2 * side
+
+        @pl.when(level >= d)
+        def _():
+            arrive(m, partner - 2 * d)
+            if share == 2:
+                act(to_twin(m, partner - 2 * d, part))
+
+        if not (isinstance(d, int) and d == 0):
+
+            @pl.when(level + d < height)
+            def _():
+                arrive(m, partner + 2 * d)
+                if share == 2:
+                    act(to_twin(m, partner + 2 * d, part))
+
+    def begin(copy):
+        copy.start()
+
+    def arrived(m, owner):
+        across(m, owner).wait_recv()
+
+    def steps(m, first, last):
+        def body(d, c):
+            relay_each(m, d, begin, arrived)
+
+            @pl.when(d > 1)
+            def _():
+                cross_each(m, d - 1, begin, arrived)
+
+            return c
+
+        lax.fori_loop(first, last, body, 0)
+
+    def gather_end(m):
+        if height > 1:
+            cross_each(m, height - 1, begin, arrived)
+        if share == 2:
+            peers(lambda d: to_twin(m, ahead(d), other).wait_recv())
+
+    loads[4].wait()
+    own_each(0, begin)
 
     def slot_at(index):
         return pl.ds(pl.multiple_of(index * slots, ROW_TILE), slots)
@@ -135,15 +224,15 @@
         return pltpu.make_async_remote_copy(
             src_ref=send.at[slot_at(peer)],
             dst_ref=recv.at[slot_at(owner)],
-            send_sem=send_sem.at[kind, peer],
-            recv_sem=recv_sem.at[kind, owner],
+            send_sem=send_sem.at[SEND_BASE + kind, peer],
+            recv_sem=recv_sem.at[RECV_BASE + kind, owner],
             device_id={"ep": peer},
             device_id_type=MESH,
         )
 
     def own_copy(kind, send, recv):
         return pltpu.make_async_copy(
-            send.at[slot_at(me)], recv.at[slot_at(me)], recv_sem.at[kind, me]
+            send.at[slot_at(me)], recv.at[slot_at(me)], recv_sem.at[RECV_BASE + kind, me]
         )
 
     def exchange_start(kind, send, recv):
@@ -154,11 +243,18 @@
         own_copy(kind, send, recv).wait()
         peers(lambda d: exchange_copy(kind, send, recv, after(d), ahead(d)).wait_recv())
 
-    ids = ids_ref[...]
-    gates = gates_ref[...]
-    choices = ids.shape[1]
+    choices = ids_ref.shape[0]
+
+    def as_column(line):
+        return jnp.transpose(jnp.broadcast_to(line, (tok_rows, tok_rows)))[:, 0:1]
+
+    ids = [
+        as_column(ids_ref[k : k + 1, :].astype(jnp.float32)).astype(jnp.int32)
+        for k in range(choices)
+    ]
+    gates = [as_column(gates_ref[k : k + 1, :]) for k in range(choices)]
     lanes = lax.broadcasted_iota(jnp.int32, (tok_rows, ep_size), 1)
-    picks = [(ids[:, k : k + 1] == lanes).astype(jnp.float32) for k in range(choices)]
+    picks = [(ids[k] == lanes).astype(jnp.float32) for k in range(choices)]
     routed = functools.reduce(jnp.add, picks)
     lower = (
         lax.broadcasted_iota(jnp.int32, (tok_rows, tok_rows), 1)
@@ -170,34 +266,35 @@
     take, place = [], []
     for k in range(choices):
         pos = jnp.sum(picks[k] * before, axis=1, keepdims=True)
-        flat = ids[:, k : k + 1].astype(jnp.float32) * slots + pos
+        flat = ids[k].astype(jnp.float32) * slots + pos
         take.append((flat.astype(jnp.int32) == by_token).astype(bf16))
         flat_row = jnp.transpose(jnp.broadcast_to(flat, (tok_rows, tok_rows)))[0:1, :]
         place.append((flat_row.astype(jnp.int32) == by_slot).astype(bf16))
 
-    def gather_wait(kind, twin_kind, src, full, first, last):
-        def arrive(d, c):
-            gather_copy(kind, src, full, ahead(d), after(d)).wait_recv()
-            if share == 2:
-                twin_copy(twin_kind, full, ahead(d), part).start()
-            return c
-
-        lax.fori_loop(first, last, arrive, 0)
-
-    def twin_wait(twin_kind, full):
-        if share == 2:
-            peers(lambda d: twin_copy(twin_kind, full, ahead(d), other).wait_recv())
-
-    gather_wait(DOWN, DOWN_TWIN, down_hbm, full_down, 1, ep_size)
+    loads[5].wait()
+    full_up[pl.ds(pl.multiple_of(me * shard, ROW_TILE), shard), :] = jnp.transpose(
+        up_shard[...].astype(jnp.float32)
+    ).astype(bf16)
+
+    steps(0, 1, 2)
+    cross_each(0, 0, begin, arrived)
+    own_each(1, begin)
+    steps(0, 2, height)
+    steps(1, 1, 2)
+    cross_each(1, 0, begin, arrived)
+    gather_end(0)
     loads[0].wait()
-    loads[4].wait()
-    twin_wait(DOWN_TWIN, full_down)
     latent = dot(tokens[...], full_down[...]).astype(bf16)
     lat_send[...] = dot(functools.reduce(jnp.add, place), latent).astype(bf16)
     exchange_start(LATENT, lat_send, lat_recv)
 
-    middle = 1 + ep_size // 2
-    gather_wait(UP, UP_TWIN, up_hbm, full_up, 1, middle)
+    steps(1, 2, height)
+    gather_end(1)
+    loads[1].wait()
+    grad_latent = dot(grad_out[...], full_up[...])
+    sent = [dot(place[k], (gates[k] * grad_latent).astype(bf16)) for k in range(choices)]
+    grad_send[...] = functools.reduce(jnp.add, sent).astype(bf16)
+    exchange_start(GRAD, grad_send, grad_recv)
 
     rows = total if total <= 512 else 256
     blocks = total // rows
@@ -224,24 +321,6 @@
     each_block(forward)
     exchange_start(FORWARD, out_send, out_recv)
 
-    gather_wait(UP, UP_TWIN, up_hbm, full_up, middle, ep_size)
-    loads[1].wait()
-    loads[5].wait()
-    twin_wait(UP_TWIN, full_up)
-    grad_latent = dot(grad_out[...], full_up[...])
-    sent = [
-        dot(place[k], (gates[:, k : k + 1] * grad_latent).astype(bf16)) for k in range(choices)
-    ]
-    grad_send[...] = functools.reduce(jnp.add, sent).astype(bf16)
-    exchange_start(GRAD, grad_send, grad_recv)
-
-    exchange_wait(FORWARD, out_send, out_recv)
-    returned = out_recv[...]
-    combined = functools.reduce(
-        jnp.add, [gates[:, k : k + 1] * dot(take[k], returned) for k in range(choices)]
-    ).astype(bf16)
-    layer_ref[...] = contract_last(combined, full_up[...]).astype(bf16)
-
     def backward(at):
         grad_act = contract_last(grad_recv[at, :], expert_down[...])
         grad_pre = (2.0 * pre_act[at, :] * grad_act).astype(bf16)
@@ -250,22 +329,42 @@
     exchange_wait(GRAD, grad_send, grad_recv)
     each_block(backward)
     exchange_start(BACKWARD, in_send, in_recv)
+
+    exchange_wait(FORWARD, out_send, out_recv)
+    returned = out_recv[...]
+    combined = functools.reduce(
+        jnp.add, [gates[k] * dot(take[k], returned) for k in range(choices)]
+    ).astype(bf16)
+    layer_ref[...] = contract_last(combined, full_up[...]).astype(bf16)
+
     exchange_wait(BACKWARD, in_send, in_recv)
     grad_sum = dot(functools.reduce(jnp.add, take), in_recv[...]).astype(bf16)
     grad_ref[...] = contract_last(grad_sum, full_down[...]).astype(bf16)
 
     def finish(d):
-        gather_copy(DOWN, down_hbm, full_down, me, after(d)).wait_send()
-        gather_copy(UP, up_hbm, full_up, me, after(d)).wait_send()
         exchange_copy(LATENT, lat_send, lat_recv, after(d), me).wait_send()
         exchange_copy(GRAD, grad_send, grad_recv, after(d), me).wait_send()
         exchange_copy(FORWARD, out_send, out_recv, after(d), me).wait_send()
         exchange_copy(BACKWARD, in_send, in_recv, after(d), me).wait_send()
-        if share == 2:
-            twin_copy(DOWN_TWIN, full_down, after(d), part).wait_send()
-            twin_copy(UP_TWIN, full_up, after(d), part).wait_send()
 
     peers(finish)
+
+    def end(copy):
+        copy.wait_send()
+
+    def nothing(m, owner):
+        del m, owner
+
+    for m in range(2):
+        own_each(m, end)
+        cross_each(m, 0, end, nothing)
+
+        def drain(d, c, m=m):
+            relay_each(m, d, end, nothing)
+            cross_each(m, d, end, nothing)
+            return c
+
+        lax.fori_loop(1, height, drain, 0)
 
 
 def on_device(
@@ -276,7 +375,7 @@
     tok_rows, model = tokens.shape
     top_count = expert_ids.shape[1]
     local_experts, width, hidden = expert_up.shape
-    assert local_experts == 1
+    assert local_experts == 1 and ep_size % 2 == 0
     experts = local_experts * ep_size
     capacity = max(2, (3 * tok_rows * top_count + 2 * experts - 1) // (2 * experts))
     slots = (capacity + ROW_TILE - 1) // ROW_TILE * ROW_TILE
@@ -299,6 +398,7 @@
             pltpu.VMEM((hidden, width), bf16),
             pltpu.VMEM((model, width), bf16),
             pltpu.VMEM((model, width), bf16),
+            pltpu.VMEM((width, shard), bf16),
             buffer,
             buffer,
             buffer,
@@ -309,19 +409,19 @@
             buffer,
             buffer,
             pltpu.SemaphoreType.DMA((6,)),
-            pltpu.SemaphoreType.DMA((8, ep_size)),
+            pltpu.SemaphoreType.DMA((12, ep_size)),
             pltpu.SemaphoreType.DMA((8, ep_size)),
         ],
         compiler_params=pltpu.CompilerParams(
             collective_id=0, has_side_effects=True, vmem_limit_bytes=60 * 1024 * 1024
         ),
     )(
-        expert_ids,
-        gate_values,
+        expert_ids.T,
+        gate_values.T,
         tokens,
         grad_out,
         latent_down,
-        latent_up.T,
+        latent_up,
         expert_up,
         expert_down,
     )

time: 104 us -> 72.2 us (0.69)
  Pallas kernels: 94.4 us -> 66.7 us
  local copies, waits for them, and re-layouts: 8.38 us -> 3.76 us
    pallas_call x1, Pallas kernels: 94.4 us -> 66.7 us  [on_device(): pl.pallas_call(functools.partial(kernel, ep_size, share, slots), out_shap...]
    unnamed x5 -> x2, local copies, waits for them, and re-layouts: 8.38 us -> 3.76 us
where the time goes in v2:
time: 72.2 us; the launch traced here: 71.1 us
  Pallas kernels  66.7 us (92%)
  local copies, waits for them, and re-layouts  3.76 us (5%)
    pallas_call x1, Pallas kernels, on_device(): pl.pallas_call(functools.partial(kernel, ep_size, share, slots), out_shap...  66.7 us
    unnamed x2, local copies, waits for them, and re-layouts  3.76 us

profile of v2, /device:TPU:0, one launch (start us, length us, event | category | flops | bytes accessed | tf_op | source)
XLA Modules:
  0.0 71.1 jit_solution(17442399646003070098)
XLA Ops:
  0.6 66.7 %shard_map.95 = (bf16[128,2048]{1,0:T(8,128)(2,1)}, bf16[128,2048]{1,0:T(8,128)(2,1)}) custom-call(s32[2,128]{1,0:T(2,128)} %bitcast.2, f32[2,128]{1,0:T(2,128)} %bitcast.3, bf16[128,2048]{1,0:T(8,128)(2,1)} %tokens_hbm.1, bf16[128,2048]{1,0:T(8,128)(2,1)} %grad_out_hbm.1, bf16[256,512]{1,0:T(8,128)(2,1)} %down_hbm.1, bf16[512,256]{1,0:T(8,128)(2,1)} %up_hbm.1, ...), custom_call_target="tpu_custom_call" | custom-call | tf_op jit(solution)/shard_map/pallas_call | solution.py:389
  67.3 1.9 %copy.12 = bf16[128,2048]{1,0:T(8,128)(2,1)} copy(bf16[128,2048]{1,0:T(8,128)(2,1)} %get-tuple-element.4) | data formatting | bytes 1048576
  69.2 1.9 %copy.13 = bf16[128,2048]{1,0:T(8,128)(2,1)} copy(bf16[128,2048]{1,0:T(8,128)(2,1)} %get-tuple-element.5) | data formatting | bytes 1048576

commit v3 on v2

--- a/solution.py
+++ b/solution.py
@@ -10,9 +10,9 @@
 MESH = pl.DeviceIdType.MESH
 ROW_TILE = 16
 
-UPWARD, DOWNWARD, ACROSS, TWIN = range(4)
+UPWARD, DOWNWARD, ACROSS, TWIN, MATE, TWIN_MATE = range(6)
 LATENT, GRAD, FORWARD, BACKWARD = range(4)
-SEND_BASE, RECV_BASE = 8, 4
+SEND_BASE, RECV_BASE = 12, 8
 
 
 def dot(left, right):
@@ -62,8 +62,11 @@
     me = lax.axis_index("ep")
     row = lax.axis_index("dp")
     twin = row + 1 - 2 * lax.rem(row, 2)
-    part = lax.rem(row, 2) if share == 2 else 0
-    other = 1 - part
+    mate = row + 2 - 4 * lax.rem(row // 2, 2)
+    part, twin_part, mate_part = [
+        lax.rem(r, 4) if share > 1 else 0 for r in (row, twin, mate)
+    ]
+    twin_mate_part = 6 - part - twin_part - mate_part
     shard = down_hbm.shape[0]
     piece = shard // share
     tok_rows = tokens.shape[0]
@@ -101,9 +104,10 @@
         pl.semaphore_signal(barrier, inc=1, device_id={"ep": after(d)}, device_id_type=MESH)
 
     peers(greet)
-    if share == 2:
+    if share > 1:
         pl.semaphore_signal(barrier, inc=1, device_id={"dp": twin}, device_id_type=MESH)
-    pl.semaphore_wait(barrier, ep_size - 1 + (share - 1))
+        pl.semaphore_signal(barrier, inc=1, device_id={"dp": mate}, device_id_type=MESH)
+    pl.semaphore_wait(barrier, ep_size - 1 + (2 if share > 1 else 0))
 
     def piece_at(owner, which):
         return pl.ds(pl.multiple_of(owner * shard + which * piece, ROW_TILE), piece)
@@ -113,12 +117,12 @@
     level = me // 2
     side = lax.rem(me, 2)
 
-    def piece_copy(m, owner, which, target, row_of, from_twin=0):
+    def piece_copy(m, owner, which, target, row_of, arrival=0):
         return pltpu.make_async_remote_copy(
             src_ref=full[m].at[piece_at(owner, which)],
             dst_ref=full[m].at[piece_at(owner, which)],
-            send_sem=send_sem.at[4 * m + row_of, owner],
-            recv_sem=recv_sem.at[2 * m + from_twin, owner],
+            send_sem=send_sem.at[6 * m + row_of, owner],
+            recv_sem=recv_sem.at[4 * m + arrival, owner],
             device_id=target,
             device_id_type=MESH,
         )
@@ -134,6 +138,17 @@
 
     def to_twin(m, owner, which):
         return piece_copy(m, owner, which, {"dp": twin}, TWIN, 1)
+
+    def to_mate(m, owner, which):
+        return piece_copy(m, owner, which, {"dp": mate}, MATE, 2)
+
+    def pass_mate(m, owner, which):
+        return piece_copy(m, owner, which, {"dp": twin}, TWIN_MATE, 3)
+
+    def share_out(m, owner, act):
+        if share > 1:
+            act(to_mate(m, owner, part))
+            act(to_twin(m, owner, part))
 
     def own_each(m, act):
         @pl.when(level + 1 < height)
@@ -157,8 +172,7 @@
                 act(upward(m, owner))
 
             act(across(m, owner))
-            if share == 2:
-                act(to_twin(m, owner, part))
+            share_out(m, owner, act)
 
         @pl.when(level + d < height)
         def _():
@@ -170,8 +184,7 @@
                 act(downward(m, owner))
 
             act(across(m, owner))
-            if share == 2:
-                act(to_twin(m, owner, part))
+            share_out(m, owner, act)
 
     def cross_each(m, d, act, arrive):
         partner = me + 1 - 2 * side
@@ -179,16 +192,14 @@
         @pl.when(level >= d)
         def _():
             arrive(m, partner - 2 * d)
-            if share == 2:
-                act(to_twin(m, partner - 2 * d, part))
+            share_out(m, partner - 2 * d, act)
 
         if not (isinstance(d, int) and d == 0):
 
             @pl.when(level + d < height)
             def _():
                 arrive(m, partner + 2 * d)
-                if share == 2:
-                    act(to_twin(m, partner + 2 * d, part))
+                share_out(m, partner + 2 * d, act)
 
     def begin(copy):
         copy.start()
@@ -211,8 +222,30 @@
     def gather_end(m):
         if height > 1:
             cross_each(m, height - 1, begin, arrived)
-        if share == 2:
-            peers(lambda d: to_twin(m, ahead(d), other).wait_recv())
+        if share > 1:
+
+            def pass_on(level_of, side_of):
+                owner = level_of * 2 + side_of
+                to_mate(m, owner, mate_part).wait_recv()
+                pass_mate(m, owner, mate_part).start()
+
+            def near(d, c):
+                @pl.when(level >= d)
+                def _():
+                    pass_on(level - d, side)
+                    pass_on(level - d, 1 - side)
+
+                @pl.when(level + d < height)
+                def _():
+                    pass_on(level + d, side)
+                    pass_on(level + d, 1 - side)
+
+                return c
+
+            pass_on(level, 1 - side)
+            lax.fori_loop(1, height, near, 0)
+            peers(lambda d: to_twin(m, ahead(d), twin_part).wait_recv())
+            peers(lambda d: pass_mate(m, ahead(d), twin_mate_part).wait_recv())
 
     loads[4].wait()
     own_each(0, begin)
@@ -346,6 +379,9 @@
         exchange_copy(GRAD, grad_send, grad_recv, after(d), me).wait_send()
         exchange_copy(FORWARD, out_send, out_recv, after(d), me).wait_send()
         exchange_copy(BACKWARD, in_send, in_recv, after(d), me).wait_send()
+        if share > 1:
+            for m in range(2):
+                pass_mate(m, after(d), mate_part).wait_send()
 
     peers(finish)
 
@@ -381,7 +417,7 @@
     slots = (capacity + ROW_TILE - 1) // ROW_TILE * ROW_TILE
     total = experts * slots
     shard = latent_down.shape[0]
-    share = 2 if dp_size % 2 == 0 and shard % (2 * ROW_TILE) == 0 else 1
+    share = 4 if dp_size % 4 == 0 and shard % (4 * ROW_TILE) == 0 else 1
     bf16 = jnp.bfloat16
     buffer = pltpu.VMEM((total, width), bf16)
     vmem = pl.BlockSpec(memory_space=pltpu.VMEM)
@@ -409,8 +445,8 @@
             buffer,
             buffer,
             pltpu.SemaphoreType.DMA((6,)),
+            pltpu.SemaphoreType.DMA((16, ep_size)),
             pltpu.SemaphoreType.DMA((12, ep_size)),
-            pltpu.SemaphoreType.DMA((8, ep_size)),
         ],
         compiler_params=pltpu.CompilerParams(
             collective_id=0, has_side_effects=True, vmem_limit_bytes=60 * 1024 * 1024

time: 72.2 us -> 69.3 us (0.960)
  the two profiles are of different devices: /device:TPU:0 before, /device:TPU:31 now
where the time goes in v3:
time: 69.3 us; the launch traced here: 69.1 us
  Pallas kernels  64.7 us (93%)
  local copies, waits for them, and re-layouts  3.76 us (5%)
    pallas_call x1, Pallas kernels, on_device(): pl.pallas_call(functools.partial(kernel, ep_size, share, slots), out_shap...  64.7 us
    unnamed x2, local copies, waits for them, and re-layouts  3.76 us

profile of v3, /device:TPU:31, one launch (start us, length us, event | category | flops | bytes accessed | tf_op | source)
XLA Modules:
  0.0 69.1 jit_solution(1113365847642668746)
XLA Ops:
  0.6 64.7 %shard_map.95 = (bf16[128,2048]{1,0:T(8,128)(2,1)}, bf16[128,2048]{1,0:T(8,128)(2,1)}) custom-call(s32[2,128]{1,0:T(2,128)} %bitcast.2, f32[2,128]{1,0:T(2,128)} %bitcast.3, bf16[128,2048]{1,0:T(8,128)(2,1)} %tokens_hbm.1, bf16[128,2048]{1,0:T(8,128)(2,1)} %grad_out_hbm.1, bf16[256,512]{1,0:T(8,128)(2,1)} %down_hbm.1, bf16[512,256]{1,0:T(8,128)(2,1)} %up_hbm.1, ...), custom_call_target="tpu_custom_call" | custom-call | tf_op jit(solution)/shard_map/pallas_call | solution.py:425
  65.3 1.9 %copy.12 = bf16[128,2048]{1,0:T(8,128)(2,1)} copy(bf16[128,2048]{1,0:T(8,128)(2,1)} %get-tuple-element.4) | data formatting | bytes 1048576
  67.2 1.9 %copy.13 = bf16[128,2048]{1,0:T(8,128)(2,1)} copy(bf16[128,2048]{1,0:T(8,128)(2,1)} %get-tuple-element.5) | data formatting | bytes 1048576

commit v4 on v3

--- a/solution.py
+++ b/solution.py
@@ -268,13 +268,41 @@
             send.at[slot_at(me)], recv.at[slot_at(me)], recv_sem.at[RECV_BASE + kind, me]
         )
 
+    half = ep_size // 2
+    near_base = me // half * half
+    far_base = half - near_base
+
+    def each_near(body):
+        lax.fori_loop(
+            1, half, lambda i, c: (body(near_base + lax.rem(me + i, half)), c)[1], 0
+        )
+
+    def each_far(body):
+        lax.fori_loop(
+            0, half, lambda i, c: (body(far_base + lax.rem(me + i, half)), c)[1], 0
+        )
+
+    def start_near(kind, send, recv):
+        each_near(lambda p: exchange_copy(kind, send, recv, p, me).start())
+        own_copy(kind, send, recv).start()
+
+    def start_far(kind, send, recv):
+        each_far(lambda p: exchange_copy(kind, send, recv, p, me).start())
+
+    def wait_near(kind, send, recv):
+        own_copy(kind, send, recv).wait()
+        each_near(lambda p: exchange_copy(kind, send, recv, p, p).wait_recv())
+
+    def wait_far(kind, send, recv):
+        each_far(lambda p: exchange_copy(kind, send, recv, p, p).wait_recv())
+
     def exchange_start(kind, send, recv):
-        peers(lambda d: exchange_copy(kind, send, recv, after(d), me).start())
-        own_copy(kind, send, recv).start()
+        start_far(kind, send, recv)
+        start_near(kind, send, recv)
 
     def exchange_wait(kind, send, recv):
-        own_copy(kind, send, recv).wait()
-        peers(lambda d: exchange_copy(kind, send, recv, after(d), ahead(d)).wait_recv())
+        wait_near(kind, send, recv)
+        wait_far(kind, send, recv)
 
     choices = ids_ref.shape[0]
 
@@ -329,19 +357,18 @@
     grad_send[...] = functools.reduce(jnp.add, sent).astype(bf16)
     exchange_start(GRAD, grad_send, grad_recv)
 
-    rows = total if total <= 512 else 256
-    blocks = total // rows
-
-    def each_block(body):
-        if blocks == 1:
-            body(slice(None))
-        else:
-            lax.fori_loop(
-                0,
-                blocks,
-                lambda b, c: (body(pl.ds(pl.multiple_of(b * rows, ROW_TILE), rows)), c)[1],
-                0,
-            )
+    rows = half * slots if half * slots <= 512 else 256
+
+    def each_block(base, body):
+        lax.fori_loop(
+            0,
+            half * slots // rows,
+            lambda b, c: (
+                body(pl.ds(pl.multiple_of(base * slots + b * rows, ROW_TILE), rows)),
+                c,
+            )[1],
+            0,
+        )
 
     def forward(at):
         hidden = jnp.maximum(dot(lat_recv[at, :], expert_up[...]), 0.0)
@@ -350,18 +377,24 @@
 
     loads[2].wait()
     loads[3].wait()
-    exchange_wait(LATENT, lat_send, lat_recv)
-    each_block(forward)
-    exchange_start(FORWARD, out_send, out_recv)
+    wait_near(LATENT, lat_send, lat_recv)
+    each_block(near_base, forward)
+    start_near(FORWARD, out_send, out_recv)
+    wait_far(LATENT, lat_send, lat_recv)
+    each_block(far_base, forward)
+    start_far(FORWARD, out_send, out_recv)
 
     def backward(at):
         grad_act = contract_last(grad_recv[at, :], expert_down[...])
         grad_pre = (2.0 * pre_act[at, :] * grad_act).astype(bf16)
         in_send[at, :] = contract_last(grad_pre, expert_up[...]).astype(bf16)
 
-    exchange_wait(GRAD, grad_send, grad_recv)
-    each_block(backward)
-    exchange_start(BACKWARD, in_send, in_recv)
+    wait_near(GRAD, grad_send, grad_recv)
+    each_block(near_base, backward)
+    start_near(BACKWARD, in_send, in_recv)
+    wait_far(GRAD, grad_send, grad_recv)
+    each_block(far_base, backward)
+    start_far(BACKWARD, in_send, in_recv)
 
     exchange_wait(FORWARD, out_send, out_recv)
     returned = out_recv[...]

time: 69.3 us -> 73 us (1.053)
  the two profiles are of different devices: /device:TPU:31 before, /device:TPU:0 now
where the time goes in v4:
time: 73 us; the launch traced here: 72.8 us
  Pallas kernels  68.4 us (94%)
  local copies, waits for them, and re-layouts  3.76 us (5%)
    pallas_call x1, Pallas kernels, on_device(): pl.pallas_call(functools.partial(kernel, ep_size, share, slots), out_shap...  68.4 us
    unnamed x2, local copies, waits for them, and re-layouts  3.76 us

profile of v4, /device:TPU:0, one launch (start us, length us, event | category | flops | bytes accessed | tf_op | source)
XLA Modules:
  0.0 72.8 jit_solution(16046531797949723675)
XLA Ops:
  0.6 68.4 %shard_map.95 = (bf16[128,2048]{1,0:T(8,128)(2,1)}, bf16[128,2048]{1,0:T(8,128)(2,1)}) custom-call(s32[2,128]{1,0:T(2,128)} %bitcast.2, f32[2,128]{1,0:T(2,128)} %bitcast.3, bf16[128,2048]{1,0:T(8,128)(2,1)} %tokens_hbm.1, bf16[128,2048]{1,0:T(8,128)(2,1)} %grad_out_hbm.1, bf16[256,512]{1,0:T(8,128)(2,1)} %down_hbm.1, bf16[512,256]{1,0:T(8,128)(2,1)} %up_hbm.1, ...), custom_call_target="tpu_custom_call" | custom-call | tf_op jit(solution)/shard_map/pallas_call | solution.py:458
  69.0 1.9 %copy.12 = bf16[128,2048]{1,0:T(8,128)(2,1)} copy(bf16[128,2048]{1,0:T(8,128)(2,1)} %get-tuple-element.4) | data formatting | bytes 1048576
  70.9 1.9 %copy.13 = bf16[128,2048]{1,0:T(8,128)(2,1)} copy(bf16[128,2048]{1,0:T(8,128)(2,1)} %get-tuple-element.5) | data formatting | bytes 1048576

commit v5 on v3

--- a/solution.py
+++ b/solution.py
@@ -322,12 +322,6 @@
     exchange_start(LATENT, lat_send, lat_recv)
 
     steps(1, 2, height)
-    gather_end(1)
-    loads[1].wait()
-    grad_latent = dot(grad_out[...], full_up[...])
-    sent = [dot(place[k], (gates[k] * grad_latent).astype(bf16)) for k in range(choices)]
-    grad_send[...] = functools.reduce(jnp.add, sent).astype(bf16)
-    exchange_start(GRAD, grad_send, grad_recv)
 
     rows = total if total <= 512 else 256
     blocks = total // rows
@@ -353,6 +347,13 @@
     exchange_wait(LATENT, lat_send, lat_recv)
     each_block(forward)
     exchange_start(FORWARD, out_send, out_recv)
+
+    gather_end(1)
+    loads[1].wait()
+    grad_latent = dot(grad_out[...], full_up[...])
+    sent = [dot(place[k], (gates[k] * grad_latent).astype(bf16)) for k in range(choices)]
+    grad_send[...] = functools.reduce(jnp.add, sent).astype(bf16)
+    exchange_start(GRAD, grad_send, grad_recv)
 
     def backward(at):
         grad_act = contract_last(grad_recv[at, :], expert_down[...])

time: 69.3 us -> 71.7 us (1.035)
  the two profiles are of different devices: /device:TPU:31 before, /device:TPU:0 now
where the time goes in v5:
time: 71.7 us; the launch traced here: 70.8 us
  Pallas kernels  66.4 us (93%)
  local copies, waits for them, and re-layouts  3.76 us (5%)
    pallas_call x1, Pallas kernels, on_device(): pl.pallas_call(functools.partial(kernel, ep_size, share, slots), out_shap...  66.4 us
    unnamed x2, local copies, waits for them, and re-layouts  3.76 us

profile of v5, /device:TPU:0, one launch (start us, length us, event | category | flops | bytes accessed | tf_op | source)
XLA Modules:
  0.0 70.8 jit_solution(3939604619784635208)
XLA Ops:
  0.6 66.4 %shard_map.95 = (bf16[128,2048]{1,0:T(8,128)(2,1)}, bf16[128,2048]{1,0:T(8,128)(2,1)}) custom-call(s32[2,128]{1,0:T(2,128)} %bitcast.2, f32[2,128]{1,0:T(2,128)} %bitcast.3, bf16[128,2048]{1,0:T(8,128)(2,1)} %tokens_hbm.1, bf16[128,2048]{1,0:T(8,128)(2,1)} %grad_out_hbm.1, bf16[256,512]{1,0:T(8,128)(2,1)} %down_hbm.1, bf16[512,256]{1,0:T(8,128)(2,1)} %up_hbm.1, ...), custom_call_target="tpu_custom_call" | custom-call | tf_op jit(solution)/shard_map/pallas_call | solution.py:426
  67.0 1.9 %copy.12 = bf16[128,2048]{1,0:T(8,128)(2,1)} copy(bf16[128,2048]{1,0:T(8,128)(2,1)} %get-tuple-element.4) | data formatting | bytes 1048576
  68.9 1.9 %copy.13 = bf16[128,2048]{1,0:T(8,128)(2,1)} copy(bf16[128,2048]{1,0:T(8,128)(2,1)} %get-tuple-element.5) | data formatting | bytes 1048576
